TPU v7x, 32 devices: a whole 2x2x4 slice. The times are simulated.
32 devices in a mesh: group: 2 (over y), expert: 8 (over z, x), tensor: 2 (over core).
Axes of the slice: x: 2, y: 2, z: 4, core: 2. Of those that a mesh axis runs over, the one named last changes fastest.
Arguments:
- tokens: bfloat16 [16, 256, 1280], P(('group', 'expert'), 'tensor'), parts along dimension 0, may hold values from -6 to 6
- ln_gain: float32 [1280], replicated, may hold values from 0.5 to 1.5
- slot_keys: bfloat16 [1280, 8], P(None, 'expert'), may hold values from -0.3125 to 0.3125
- w_gate: bfloat16 [8, 1280, 1280], P('expert', 'tensor'), may hold values from -0.15625 to 0.15625
- w_up: bfloat16 [8, 1280, 1280], P('expert', 'tensor'), may hold values from -0.15625 to 0.15625
- w_down: bfloat16 [8, 1280, 1280], P('expert', 'tensor'), may hold values from -0.25 to 0.25
Outputs:
- output: bfloat16 [16, 256, 1280], P(('group', 'expert'), 'tensor'), parts along dimension 0
There are 2 independent parts, one for each index of `group`. A program takes and returns all parts, laid end to end along the dimension named above; an argument that names none is the same for every part. Nothing has to cross between parts.
All inputs are finite; a program needn't handle non-finite values.
Results may differ from a plain program's by a relative error of at most 0.0034.
Values may be sent and summed in bfloat16 or wider, within the bound.
No kernel may reach another device: no remote copies, remote signals or barrier semaphores. Data moves between devices by JAX's collectives and lax.ppermute only.
A program may use at most 64 MiB of HBM per device.

v0:
```python
import jax
import jax.numpy as jnp
from jax import lax
from jax.sharding import PartitionSpec as P

epsilon = 1e-06
soft_cap = 20.0


def layer_norm(tokens, ln_gain):
    widened = tokens.astype(jnp.float32)
    center = widened - jnp.mean(widened, axis=-1, keepdims=True)
    variance = jnp.mean(center * center, axis=-1, keepdims=True)
    return (center * lax.rsqrt(variance + epsilon) * ln_gain).astype(jnp.bfloat16)


def on_device(tokens, ln_gain, slot_keys, w_gate, w_up, w_down):
    tensor_count = lax.axis_size("tensor")
    img_dev, half_patches, model_width = tokens.shape
    all_keys = lax.all_gather(slot_keys, "expert", axis=1, tiled=True)
    slot_count = all_keys.shape[1]
    normed = layer_norm(tokens, ln_gain)
    raw_scores = jnp.dot(
        normed.reshape(-1, model_width), all_keys, preferred_element_type=jnp.float32
    )
    raw_scores = raw_scores.reshape(img_dev, half_patches, slot_count)
    scores = jnp.exp(soft_cap * jnp.tanh(raw_scores / soft_cap))
    slot_num = jnp.einsum(
        "ips,ipd->isd", scores.astype(jnp.bfloat16), normed, preferred_element_type=jnp.float32
    )
    column_total = jnp.sum(scores, axis=1)
    combine = (scores / jnp.sum(scores, axis=2, keepdims=True)).astype(jnp.bfloat16)
    column_copies = jnp.broadcast_to(column_total[:, :, None], (img_dev, slot_count, tensor_count))
    slot_num, column_share = (
        lax.psum_scatter(slot_num, "tensor", scatter_dimension=2, tiled=True),
        lax.psum_scatter(column_copies, "tensor", scatter_dimension=2, tiled=True),
    )
    slot_in = (slot_num / column_share).astype(jnp.bfloat16)
    share_width = slot_in.shape[2]
    grouped = slot_in.reshape(img_dev, slot_count // 2, 1, 2, share_width)
    doubled = jnp.broadcast_to(grouped, (img_dev, slot_count // 2, 2, 2, share_width))
    doubled = doubled.reshape(img_dev, slot_count, 2, share_width)
    arrived = lax.all_to_all(doubled, "expert", split_axis=1, concat_axis=0, tiled=True)
    expert_in = jnp.transpose(arrived[:, 0], (1, 0, 2))
    expert_in = lax.all_gather(expert_in, "tensor", axis=2, tiled=True)
    images = expert_in.shape[1]
    flat_rows = expert_in.reshape(2 * images, model_width)
    contract = (((1,), (1,)), ((), ()))
    gate_act = lax.dot_general(flat_rows, w_gate[0], contract, preferred_element_type=jnp.float32)
    up_proj = lax.dot_general(flat_rows, w_up[0], contract, preferred_element_type=jnp.float32)
    hidden = (jax.nn.silu(gate_act) * up_proj).astype(jnp.bfloat16)
    part_out = jnp.dot(hidden, w_down[0], preferred_element_type=jnp.float32).reshape(
        2, images, model_width
    )
    summed = lax.psum_scatter(part_out, "tensor", scatter_dimension=2, tiled=True)
    outgoing = jnp.transpose(summed, (1, 0, 2))[:, None]
    returned = lax.all_to_all(outgoing, "expert", split_axis=0, concat_axis=1, tiled=True)
    paired = returned.reshape(img_dev, slot_count // 2, 2, 2, share_width)
    slot_back = (
        jnp.sum(paired, axis=2).reshape(img_dev, slot_count, share_width).astype(jnp.bfloat16)
    )
    slot_back = lax.all_gather(slot_back, "tensor", axis=2, tiled=True)
    mixed_rows = jnp.einsum("ips,isd->ipd", combine, slot_back, preferred_element_type=jnp.float32)
    return (tokens.astype(jnp.float32) + mixed_rows).astype(jnp.bfloat16)


def solution(mesh):
    placed = (
        P(("group", "expert"), "tensor", None),
        P(),
        P(None, "expert"),
        P("expert", "tensor", None),
        P("expert", "tensor", None),
        P("expert", "tensor", None),
    )
    return jax.shard_map(
        on_device,
        mesh=mesh,
        in_specs=placed,
        out_specs=P(("group", "expert"), "tensor", None),
        check_vma=False,
    )
```

profile of v0, /device:TPU:0, one launch (start us, length us, event | category | flops | bytes accessed | tf_op | source)
XLA Modules:
  0.0 98.8 jit_solution(4789264857680236152)
XLA Ops:
  6.5 0.0 copy-start
  6.5 0.0 copy-start.3
  6.5 0.0 copy-start.2
  6.5 0.0 reduce-scatter.4.cloned.1.call-start
  6.5 1.2 %convert_reduce_fusion = f32[128]{0:T(128)S(1)} fusion(bf16[1,128,1280]{2,1,0:T(8,128)(2,1)} %param.6), kind=kLoop, calls=%fused_computation.18 | loop fusion | flops 327552 | bytes 328192 | tf_op jit(solution)/shard_map/reduce_sum | solution.py:12
  7.8 1.2 %fusion.24 = f32[128]{0:T(128)S(1)} fusion(bf16[1,128,1280]{2,1,0:T(8,128)(2,1)} %param.6, f32[128]{0:T(128)S(1)} %broadcast_multiply_fusion), kind=kLoop, calls=%fused_computation.21 | loop fusion | flops 655232 | bytes 328704 | tf_op jit(solution)/shard_map/reduce_sum | solution.py:13
  9.0 32.7 %all-gather = bf16[8,1,1280]{2,1,0:T(2,128)(2,1)S(1)} all-gather(bf16[1,1,1280]{2,1,0:T(2,128)(2,1)} %bitcast.70), channel_id=1, replica_groups=mesh['group'=2,'expert'=8,'tensor'=2] {'expert'}, dimensions={0}, use_global_device_ids=true | all-gather | bytes 23040 | tf_op jit(solution)/shard_map/all_gather | solution.py:20
  41.7 1.2 %fusion.27 = bf16[128,1280]{1,0:T(8,128)(2,1)S(1)} fusion(bf16[1,128,1280]{2,1,0:T(8,128)(2,1)} %param.6, f32[1280]{0:T(1024)} %param.7, f32[128]{0:T(128)S(1)} %add_rsqrt_fusion, f32[128]{0:T(128)S(1)} %broadcast_multiply_fusion), kind=kLoop, calls=%fused_computation.24 | loop fusion | flops 819200 | bytes 661504 | tf_op jit(solution)/shard_map/reshape | solution.py:24
  43.0 0.3 fusion.43
  43.3 0.8 convolution_bitcast_fusion.1
  44.1 0.0 reduce-scatter.4.cloned.1.call-update
  44.1 0.0 reduce-scatter.6.cloned.1.call-start
  44.2 2.5 %all-reduce = f32[1,8,2]{1,2,0:T(2,128)S(1)} all-reduce(f32[1,8,2]{1,2,0:T(2,128)S(1)} %broadcast_in_dim.10), channel_id=3, replica_groups=mesh['group'=2,'expert'=8,'tensor'=2] {'tensor'}, use_global_device_ids=true, to_apply=%region_5.0.clone | all-reduce | flops 16 | bytes 128
  46.6 0.0 copy-done.3
  46.7 0.6 dynamic-slice
  47.3 0.6 dynamic-slice_bitcast_fusion
  47.9 4.7 %reduce-scatter.4.cloned.1.call-done = f32[1,8,640]{2,1,0:T(8,128)} async-done(((f32[1,8,1280]{2,1,0:T(8,128)}), f32[1,8,640]{2,1,0:T(8,128)}) %reduce-scatter.4.cloned.1.call-update) | async-done | bytes 20496 | tf_op jit(solution)/shard_map/reduce_scatter | solution.py:35
  52.6 0.8 divide_convert_fusion
  53.4 12.1 %all_to_all.8 = bf16[1,8,2,640]{3,2,0,1:T(2,128)(2,1)S(1)} all-to-all(bf16[1,8,2,640]{3,2,0,1:T(2,128)(2,1)S(1)} %bitcast.67), channel_id=1, replica_groups=mesh['group'=2,'expert'=8,'tensor'=2] {'expert'}, dimensions={1} | all-to-all | bytes 40960 | tf_op jit(solution)/shard_map/all_to_all | solution.py:43
  65.6 1.8 %all_gather.10 = bf16[2,8,1280]{2,1,0:T(8,128)(2,1)S(1)} all-gather(bf16[2,8,640]{2,1,0:T(8,128)(2,1)S(1)} %bitcast.68), channel_id=1, replica_groups=mesh['group'=2,'expert'=8,'tensor'=2] {'tensor'}, dimensions={2}, use_global_device_ids=true | all-gather | bytes 61440 | tf_op jit(solution)/shard_map/all_gather | solution.py:45
  67.4 0.0 copy-done.2
  67.4 0.5 fusion.6
  67.9 0.0 copy-done
  67.9 0.0 copy-start.1
  67.9 3.0 %fusion.2 = f32[2,8,1280]{2,1,0:T(8,128)} fusion(bf16[1,640,1280]{2,1,0:T(8,128)(2,1)S(1)} %copy-done, bf16[1,640,1280]{2,1,0:T(8,128)(2,1)} %param.10, bf16[2,8,1280]{2,1,0:T(8,128)(2,1)S(1)} %all_gather.10, f32[16,640]{1,0:T(8,128)S(1)} %fusion.6), kind=kOutput, calls=%fused_computation.4 | convolution fusion | flops 52490240 | bytes 3440640 | tf_op jit(solution)/shard_map/dot_general | solution.py:52
  71.0 0.0 reduce-scatter.6.cloned.1.call-update
  71.0 5.0 %reduce-scatter.6.cloned.1.call-done = f32[2,8,640]{2,1,0:T(8,128)} async-done(((f32[2,8,1280]{2,1,0:T(8,128)}), f32[2,8,640]{2,1,0:T(8,128)}) %reduce-scatter.6.cloned.1.call-update) | async-done | bytes 40976 | tf_op jit(solution)/shard_map/reduce_scatter | solution.py:55
  76.0 0.8 copy.12
  76.8 12.2 %all_to_all.9 = f32[8,1,2,640]{3,2,1,0:T(2,128)S(1)} all-to-all(f32[8,1,2,640]{3,2,1,0:T(2,128)S(1)} %copy.12), channel_id=1, replica_groups=mesh['group'=2,'expert'=8,'tensor'=2] {'expert'}, dimensions={0} | all-to-all | bytes 81920 | tf_op jit(solution)/shard_map/all_to_all | solution.py:57
  89.1 1.8 %all_gather.11 = bf16[1,8,1280]{2,1,0:T(8,128)(2,1)S(1)} all-gather(bf16[1,8,640]{2,1,0:T(8,128)(2,1)S(1)} %convert_element_type.45), channel_id=1, replica_groups=mesh['group'=2,'expert'=8,'tensor'=2] {'tensor'}, dimensions={2}, use_global_device_ids=true | all-gather | bytes 30720 | tf_op jit(solution)/shard_map/all_gather | solution.py:62
  91.0 0.0 copy-done.1
  91.0 1.0 %fusion.1 = bf16[1,128,1280]{2,1,0:T(8,128)(2,1)} fusion(bf16[1,128,1280]{2,1,0:T(8,128)(2,1)S(1)} %copy-done.1, bf16[1,8,1280]{2,1,0:T(8,128)(2,1)S(1)} %all_gather.11, f32[128,8]{0,1:T(8,128)S(1)} %get-tuple-element.7, f32[128]{0:T(128)S(1)} %get-tuple-element.5), kind=kOutput, calls=%fused_computation.2 | convolution fusion | flops 3115008 | bytes 680448 | tf_op jit(solution)/shard_map/ips,isd->ipd/dot_general | solution.py:63
  (10 shorter events, 0.1 us)
Async XLA Ops:
  6.5 61.4 %copy-start = (bf16[1,640,1280]{2,1,0:T(8,128)(2,1)S(1)}, bf16[1,640,1280]{2,1,0:T(8,128)(2,1)}, u32[]{:S(2)}) copy-start(bf16[1,640,1280]{2,1,0:T(8,128)(2,1)} %param.11) | copy-start | bytes 4915204
  6.5 40.1 %copy-start.3 = (u32[32]{0:T(128)S(1)}, u32[32]{0:T(128)}, u32[]{:S(2)}) copy-start(u32[32]{0:T(128)} %constant.22) | copy-start | bytes 388
  6.5 60.9 %copy-start.2 = (bf16[1,640,1280]{2,1,0:T(8,128)(2,1)S(1)}, bf16[1,640,1280]{2,1,0:T(8,128)(2,1)}, u32[]{:S(2)}) copy-start(bf16[1,640,1280]{2,1,0:T(8,128)(2,1)} %param.9) | copy-start | bytes 4915204
  6.5 46.1 %reduce-scatter.4.cloned.1.call-start = ((), (), s32[]{:S(2)}) async-start(), calls=%async_computation.4 | async-start | bytes 61440 | tf_op jit(solution)/shard_map/reduce_scatter | solution.py:35
  44.1 31.9 %reduce-scatter.6.cloned.1.call-start = ((), (), s32[]{:S(2)}) async-start(), calls=%async_computation.5 | async-start | bytes 122880 | tf_op jit(solution)/shard_map/reduce_scatter | solution.py:55
  67.9 23.0 %copy-start.1 = (bf16[1,128,1280]{2,1,0:T(8,128)(2,1)S(1)}, bf16[1,128,1280]{2,1,0:T(8,128)(2,1)}, u32[]{:S(2)}) copy-start(bf16[1,128,1280]{2,1,0:T(8,128)(2,1)} %param.6) | copy-start | bytes 983044
Sparse Core Ops, SparseCore 0:
  44.2 8.3 reduce-scatter.3
  71.1 4.8 reduce-scatter.5
where the time goes:
time: 99.2 us; the launch traced here: 98.8 us
  blocking collectives  63.2 us (64%)
  between operations  13.5 us (14%)
  waiting for transfers between devices  9.78 us (10%)
  matrix products  5.71 us (6%)
  other arithmetic  4.49 us (5%)
  local copies, waits for them, and re-layouts  2.13 us (2%)
    all_gather x1, blocking collectives, on_device(): all_keys = lax.all_gather(slot_keys, 'expert', axis=1, tiled=True)  32.7 us
    all_to_all x1, blocking collectives, on_device(): lax.all_to_all(outgoing, 'expert', split_axis=0, concat_axis=1, tiled=True)  12.2 us
    all_to_all x1, blocking collectives, on_device(): lax.all_to_all(doubled, 'expert', split_axis=1, concat_axis=0, tiled=True)  12.1 us
    reduce_scatter x1, waiting for transfers between devices, on_device(): lax.psum_scatter(part_out, 'tensor', scatter_dimension=2, tiled=True)  5.04 us
    reduce_scatter x1, waiting for transfers between devices, on_device(): lax.psum_scatter(slot_num, 'tensor', scatter_dimension=2, tiled=True)  4.7 us
    dot_general x1, matrix products, on_device(): jnp.dot(hidden, w_down[0], preferred_element_type=jnp.float32)  3.04 us
    unnamed x1, blocking collectives  2.47 us
  transfers between devices with their start and end apart: 2, of which 2 were waited for; matrix products, arithmetic and copies ran while one was open for 1% of the time, Pallas kernels for 0%

commit v1 on v0

v1 whole, which is shorter than its diff:
```python
import jax
import jax.numpy as jnp
from jax import lax
from jax.sharding import PartitionSpec as P

epsilon = 1e-06
soft_cap = 20.0
per_expert = 2
halves = 2
lanes = 128
everyone = ("expert", "tensor")


def layer_norm(tokens, ln_gain):
    widened = tokens.astype(jnp.float32)
    center = widened - jnp.mean(widened, axis=-1, keepdims=True)
    variance = jnp.mean(center * center, axis=-1, keepdims=True)
    return (center * lax.rsqrt(variance + epsilon) * ln_gain).astype(jnp.bfloat16)


def gather_keys(slot_keys):
    devices = lax.axis_size("expert")
    own = slot_keys.T[None]
    copies = jnp.broadcast_to(own, (devices,) + own.shape[1:])
    arrived = lax.all_to_all(copies, "expert", split_axis=0, concat_axis=0, tiled=True)
    return arrived.reshape(-1, slot_keys.shape[0])


def on_device(tokens, ln_gain, slot_keys, w_gate, w_up, w_down):
    tensor_count = lax.axis_size("tensor")
    devices = lax.axis_size("expert")
    img_dev, half_patches, width = tokens.shape
    all_keys = gather_keys(slot_keys)
    slot_count = all_keys.shape[0]
    experts = slot_count // per_expert
    normed = layer_norm(tokens, ln_gain)
    raw_scores = jnp.einsum("ipd,sd->ips", normed, all_keys, preferred_element_type=jnp.float32)
    scores = jnp.exp(soft_cap * jnp.tanh(raw_scores / soft_cap))
    slot_num = jnp.einsum(
        "ips,ipd->isd", scores.astype(jnp.bfloat16), normed, preferred_element_type=jnp.float32
    )
    column_total = jnp.sum(scores, axis=1)
    combine = (scores / jnp.sum(scores, axis=2, keepdims=True)).astype(jnp.bfloat16)

    coarse = column_total.astype(jnp.bfloat16)
    fine = (column_total - coarse.astype(jnp.float32)).astype(jnp.bfloat16)
    totals = jnp.broadcast_to(coarse[:, :, None], (img_dev, slot_count, lanes // 2))
    rests = jnp.broadcast_to(fine[:, :, None], (img_dev, slot_count, lanes // 2))
    message = jnp.concatenate([slot_num.astype(jnp.bfloat16), totals, rests], axis=2)
    message = message.reshape(img_dev, experts, per_expert, width + lanes)
    message = jnp.transpose(message, (1, 0, 2, 3))[:, None]
    copies = devices * tensor_count // experts
    message = jnp.broadcast_to(message, (experts, copies) + message.shape[2:])
    message = message.reshape(devices * tensor_count, img_dev * per_expert, width + lanes)
    arrived = lax.all_to_all(message, everyone, split_axis=0, concat_axis=0, tiled=True)
    arrived = arrived.reshape(devices, tensor_count, img_dev * per_expert, width + lanes)
    summed = jnp.sum(arrived.astype(jnp.float32), axis=1).reshape(-1, width + lanes)
    total = summed[:, width : width + 1] + summed[:, width + lanes // 2 : width + lanes // 2 + 1]
    rows = (summed[:, :width] / total).astype(jnp.bfloat16)

    contract = (((1,), (1,)), ((), ()))
    gate_act = lax.dot_general(rows, w_gate[0], contract, preferred_element_type=jnp.float32)
    up_proj = lax.dot_general(rows, w_up[0], contract, preferred_element_type=jnp.float32)
    hidden = (jax.nn.silu(gate_act) * up_proj).astype(jnp.bfloat16)
    part_out = jnp.dot(hidden, w_down[0], preferred_element_type=jnp.float32).astype(jnp.bfloat16)

    outgoing = part_out.reshape(devices, 1, img_dev * per_expert, width)
    outgoing = jnp.broadcast_to(outgoing, (devices, tensor_count) + outgoing.shape[2:])
    outgoing = outgoing.reshape(devices * tensor_count, img_dev * per_expert, width)
    returned = lax.all_to_all(outgoing, everyone, split_axis=0, concat_axis=0, tiled=True)
    returned = returned.reshape(experts, copies, img_dev, per_expert, width)
    slot_back = jnp.sum(returned.astype(jnp.float32), axis=1).astype(jnp.bfloat16)
    slot_back = jnp.transpose(slot_back, (1, 0, 2, 3)).reshape(img_dev, slot_count, width)
    mixed_rows = jnp.einsum("ips,isd->ipd", combine, slot_back, preferred_element_type=jnp.float32)
    return (tokens.astype(jnp.float32) + mixed_rows).astype(jnp.bfloat16)


def solution(mesh):
    placed = (
        P(("group", "expert"), "tensor", None),
        P(),
        P(None, "expert"),
        P("expert", "tensor", None),
        P("expert", "tensor", None),
        P("expert", "tensor", None),
    )
    return jax.shard_map(
        on_device,
        mesh=mesh,
        in_specs=placed,
        out_specs=P(("group", "expert"), "tensor", None),
        check_vma=False,
    )
```

time: 99.2 us -> 43.8 us (0.44)
  blocking collectives: 63.2 us -> 19.8 us
  between operations: 13.5 us -> 0.09 us
  starting transfers between devices: 0.04 us -> 7.28 us
  waiting for transfers between devices: 9.78 us -> 3.07 us
  other arithmetic: 4.49 us -> 5.49 us
    all_gather x3 -> x0, blocking collectives: 36.4 us -> none  [the longest x1 32.7 us: on_device(): all_keys = lax.all_gather(slot_keys, 'expert', axis=1, tiled=True)]
    reduce_scatter x2 -> x0, waiting for transfers between devices: 9.75 us -> none  [the longest x1 5.04 us: on_device(): lax.psum_scatter(part_out, 'tensor', scatter_dimension=2, tiled=True)]
    all_to_all x0 -> x1, starting transfers between devices: none -> 7.28 us  [gather_keys(): lax.all_to_all(copies, 'expert', split_axis=0, concat_axis=0, tiled=True)]
    all_to_all x2, blocking collectives: 24.4 us -> 19.8 us  [the longest x1 10.1 us: on_device(): lax.all_to_all(message, everyone, split_axis=0, concat_axis=0, tiled=True)]
    all_to_all x0 -> x1, waiting for transfers between devices: none -> 3.07 us  [gather_keys(): lax.all_to_all(copies, 'expert', split_axis=0, concat_axis=0, tiled=True)]
    unnamed x1 -> x0, blocking collectives: 2.47 us -> none
    dot_general x2, matrix products: 0.86 us -> 2.3 us  [the longest x1 1.97 us: on_device(): lax.dot_general(rows, w_gate[0], contract, preferred_element_type=jnp.flo...]
    another operation x0 -> x1, other arithmetic: none -> 1.21 us
  transfers between devices with their start and end apart: 2 -> 1, of which waited for: 2 -> 1; matrix products, arithmetic and copies ran while one was open for 1% -> 8% of each run, Pallas kernels for 0% -> 0%
where the time goes in v1:
time: 43.8 us; the launch traced here: 43.3 us
  blocking collectives  19.8 us (45%)
  starting transfers between devices  7.28 us (17%)
  matrix products  5.86 us (13%)
  other arithmetic  5.49 us (13%)
  waiting for transfers between devices  3.07 us (7%)
  local copies, waits for them, and re-layouts  1.76 us (4%)
    all_to_all x1, blocking collectives, on_device(): lax.all_to_all(message, everyone, split_axis=0, concat_axis=0, tiled=True)  10.1 us
    all_to_all x1, blocking collectives, on_device(): lax.all_to_all(outgoing, everyone, split_axis=0, concat_axis=0, tiled=True)  9.7 us
    all_to_all x1, starting transfers between devices, gather_keys(): lax.all_to_all(copies, 'expert', split_axis=0, concat_axis=0, tiled=True)  7.28 us
    all_to_all x1, waiting for transfers between devices, gather_keys(): lax.all_to_all(copies, 'expert', split_axis=0, concat_axis=0, tiled=True)  3.07 us
    dot_general x1, matrix products, on_device(): jnp.dot(hidden, w_down[0], preferred_element_type=jnp.float32)  2.38 us
    dot_general x1, matrix products, on_device(): lax.dot_general(rows, w_gate[0], contract, preferred_element_type=jnp.flo...  1.97 us
    reduce_sum x1, other arithmetic, layer_norm(): variance = jnp.mean(center * center, axis=-1, keepdims=True)  1.21 us
    another operation x1, other arithmetic  1.21 us
  transfers between devices with their start and end apart: 1, of which 1 were waited for; matrix products, arithmetic and copies ran while one was open for 8% of the time, Pallas kernels for 0%

profile of v1, /device:TPU:0, one launch (start us, length us, event | category | flops | bytes accessed | tf_op | source)
XLA Modules:
  0.0 43.3 jit_solution(16920953759021097762)
XLA Ops:
  0.0 0.0 copy-start
  0.0 0.8 %reduce.8 = bf16[1280]{0:T(1024)(128)(2,1)S(1)} reduce(bf16[1280,1]{0,1:T(2,128)(2,1)} %param.8, bf16[]{:T(256)} %constant.22), dimensions={1}, to_apply=%param.8.reduce_sub_computation | reduce | bytes 5122 | tf_op args[2]
  0.9 0.5 %broadcast.55 = bf16[]{:T(256)} broadcast(bf16[]{:T(256)} %constant.22), dimensions={} | broadcast | bytes 4 | tf_op jit(solution)/shard_map/broadcast_in_dim | solution.py:24
  1.4 0.8 %reduce.11 = bf16[8,1280]{1,0:T(8,128)(2,1)S(1)} reduce(bf16[8,1,1280]{2,1,0:T(2,128)(2,1)S(1)} %broadcast_in_dim.19, bf16[]{:T(256)} %broadcast.55), dimensions={1}, to_apply=%broadcast_in_dim.19.reduce_sub_computation | reduce | bytes 40962 | tf_op jit(solution)/shard_map/broadcast_in_dim | solution.py:24
  2.1 0.6 %reshape.123 = bf16[8,2,640]{2,1,0:T(2,128)(2,1)} reshape(bf16[8,1280]{1,0:T(8,128)(2,1)S(1)} %reduce.11) | data formatting | bytes 40960
  2.8 7.3 %all-to-all-start = ((bf16[8,2,640]{2,1,0:T(2,128)(2,1)}), bf16[8,2,640]{2,1,0:T(2,128)(2,1)S(1)}, u32[]{:S(2)}, u32[]{:S(2)}) async-start(bf16[8,2,640]{2,1,0:T(2,128)(2,1)} %reshape.123), calls=%async_computation | async-start | bytes 40960 | tf_op jit(solution)/shard_map/all_to_all | solution.py:25
  10.0 1.1 %convert_reduce_fusion = f32[128]{0:T(128)S(1)} fusion(bf16[1,128,1280]{2,1,0:T(8,128)(2,1)} %param.6), kind=kLoop, calls=%fused_computation.17 | loop fusion | flops 327552 | bytes 328192 | tf_op jit(solution)/shard_map/reduce_sum | solution.py:16
  11.2 1.2 %fusion.20 = f32[128]{0:T(128)S(1)} fusion(bf16[1,128,1280]{2,1,0:T(8,128)(2,1)} %param.6, f32[128]{0:T(128)S(1)} %broadcast_multiply_fusion), kind=kLoop, calls=%fused_computation.20 | loop fusion | flops 655232 | bytes 328704 | tf_op jit(solution)/shard_map/reduce_sum | solution.py:17
  12.4 1.2 %fusion.23 = bf16[128,1280]{1,0:T(8,128)(2,1)S(1)} fusion(bf16[1,128,1280]{2,1,0:T(8,128)(2,1)} %param.6, f32[1280]{0:T(1024)} %param.7, f32[128]{0:T(128)S(1)} %add_rsqrt_fusion, f32[128]{0:T(128)S(1)} %broadcast_multiply_fusion), kind=kLoop, calls=%fused_computation.23 | loop fusion | flops 819200 | bytes 661504 | tf_op jit(solution)/shard_map/reshape.4
  13.6 3.1 %all-to-all-done = bf16[8,2,640]{2,1,0:T(2,128)(2,1)S(1)} async-done(((bf16[8,2,640]{2,1,0:T(2,128)(2,1)}), bf16[8,2,640]{2,1,0:T(2,128)(2,1)S(1)}, u32[]{:S(2)}, u32[]{:S(2)}) %all-to-all-start) | async-done | bytes 20512 | tf_op jit(solution)/shard_map/all_to_all | solution.py:25
  16.7 0.3 fusion.40
  17.0 0.2 convolution_convert_fusion.1
  17.2 0.1 reduce_sum.63
  17.3 0.1 broadcast_in_dim.42
  17.4 0.1 broadcast_in_dim.20
  17.4 0.1 concatenate.7
  17.5 0.1 broadcast_in_dim.44
  17.6 10.1 %all_to_all.15 = bf16[16,2,1408]{2,1,0:T(2,128)(2,1)S(1)} all-to-all(bf16[16,2,1408]{2,1,0:T(2,128)(2,1)S(1)} %bitcast.39), channel_id=1, replica_groups=mesh['group'=2,'expert'=8,'tensor'=2] {'expert','tensor'}, dimensions={0} | all-to-all | bytes 180224 | tf_op jit(solution)/shard_map/all_to_all | solution.py:55
  27.7 0.1 convert_reduce_fusion.1
  27.8 0.1 reshape.116
  27.9 0.2 fusion.33
  28.1 2.0 %fusion.5 = f32[16,640]{1,0:T(8,128)S(1)} fusion(bf16[1,640,1280]{2,1,0:T(8,128)(2,1)} %param.9, f32[16,1408]{1,0:T(8,128)S(1)} %reshape.116, f32[16]{0:T(128)S(1)} %fusion.33), kind=kOutput, calls=%fused_computation.8 | convolution fusion | flops 26255360 | bytes 1761792 | tf_op jit(solution)/shard_map/dot_general | solution.py:62
  30.0 0.0 copy-done
  30.0 0.0 copy-start.1
  30.0 2.4 %convolution_convert_fusion = bf16[16,1280]{1,0:T(8,128)(2,1)S(1)} fusion(bf16[1,640,1280]{2,1,0:T(8,128)(2,1)S(1)} %copy-done, bf16[1,640,1280]{2,1,0:T(8,128)(2,1)} %param.10, f32[16,640]{1,0:T(8,128)S(1)} %fusion.5, f32[16,1408]{1,0:T(8,128)S(1)} %reshape.116, f32[16]{0:T(128)S(1)} %fusion.33), kind=kOutput, calls=%fused_computation.3 | convolution fusion | flops 52551680 | bytes 3441152 | tf_op jit(solution)/shard_map/dot_general | solution.py:65
  32.5 9.7 %all_to_all.16 = bf16[16,2,1280]{2,1,0:T(2,128)(2,1)S(1)} all-to-all(bf16[16,2,1280]{2,1,0:T(2,128)(2,1)S(1)} %bitcast.40), channel_id=1, replica_groups=mesh['group'=2,'expert'=8,'tensor'=2] {'expert','tensor'}, dimensions={0} | all-to-all | bytes 163840 | tf_op jit(solution)/shard_map/all_to_all | solution.py:70
  42.2 0.1 bitcast_reduce_fusion
  42.3 0.0 copy-done.1
  42.3 1.0 %fusion.1 = bf16[1,128,1280]{2,1,0:T(8,128)(2,1)} fusion(bf16[8,1280]{1,0:T(8,128)(2,1)S(1)} %reshape.119, bf16[1,128,1280]{2,1,0:T(8,128)(2,1)S(1)} %copy-done.1, f32[128,8]{0,1:T(8,128)S(1)} %get-tuple-element.9, f32[128]{0:T(128)S(1)} %get-tuple-element.5), kind=kOutput, calls=%fused_computation.2 | convolution fusion | flops 3115008 | bytes 680448 | tf_op jit(solution)/shard_map/ips,isd->ipd/dot_general | solution.py:74
  (9 shorter events, 0.2 us)
Async XLA Ops:
  0.0 30.0 %copy-start = (bf16[1,640,1280]{2,1,0:T(8,128)(2,1)S(1)}, bf16[1,640,1280]{2,1,0:T(8,128)(2,1)}, u32[]{:S(2)}) copy-start(bf16[1,640,1280]{2,1,0:T(8,128)(2,1)} %param.11) | copy-start | bytes 4915204
  2.8 13.9 %all-to-all-start = ((bf16[8,2,640]{2,1,0:T(2,128)(2,1)}), bf16[8,2,640]{2,1,0:T(2,128)(2,1)S(1)}, u32[]{:S(2)}, u32[]{:S(2)}) async-start(bf16[8,2,640]{2,1,0:T(2,128)(2,1)} %reshape.123), calls=%async_computation | async-start | bytes 40960 | tf_op jit(solution)/shard_map/all_to_all | solution.py:25
  30.0 12.3 %copy-start.1 = (bf16[1,128,1280]{2,1,0:T(8,128)(2,1)S(1)}, bf16[1,128,1280]{2,1,0:T(8,128)(2,1)}, u32[]{:S(2)}) copy-start(bf16[1,128,1280]{2,1,0:T(8,128)(2,1)} %param.6) | copy-start | bytes 983044
